TPU v7x, 256 devices: a whole 4x4x8 slice. The times are simulated.
256 devices in a mesh: batch: 2 (over core), neuron: 128 (over z, y, x).
Axes of the slice: x: 4, y: 4, z: 8, core: 2. Of those that a mesh axis runs over, the one named last changes fastest.
Arguments:
- images: bfloat16 [32, 65536], P('batch', 'neuron'), parts along dimension 0, may hold values from 0 to 32
- tile_weights: bfloat16 [2, 16384, 128, 128], P(None, 'neuron'), may hold values from -0.375 to 0.375
- tile_blocks: int32 [2, 16384, 2], P(None, 'neuron'), may hold values from 0 to 511, as said below
- tile_count: int32 [2, 128], P(None, 'neuron'), may hold values from 96 to 128, as said below
- bias: float32 [2, 65536], P(None, 'neuron'), may hold values from -48 to 48
Outputs:
- activity: bfloat16 [32, 65536], P('batch', 'neuron'), parts along dimension 0
There are 2 independent parts, one for each index of `batch`. A program takes and returns all parts, laid end to end along the dimension named above; an argument that names none is the same for every part. Nothing has to cross between parts.
Inputs may be any that keep to these rules, and one draw needn't show every extreme that they name: Slots 0 to tile_count[l, d] - 1 of device d are live in layer l; in every layer one device has all 128 live. `tile_blocks`: entry [l, d * 128 + s, :] is the row block and column block of slot s of device d. Within one device and layer the column blocks are all different, and at most 2 of them lie among the 4 column blocks of any one neuron device; in every layer the column blocks of some neuron device get exactly 2 live slots from every device.
All inputs are finite; a program needn't handle non-finite values.
Results may differ from a plain program's by a relative error of at most 0.0033.
Values may be sent and summed in bfloat16 or wider, within the bound.
No kernel may reach another device: no remote copies, remote signals or barrier semaphores. Data moves between devices by JAX's collectives and lax.ppermute only.
A program may use at most 64 MiB of HBM per device.

v0:
```python
import jax
import jax.numpy as jnp
from jax import lax
from jax.sharding import Mesh
from jax.sharding import PartitionSpec as P

NEURON = ("neuron_0", "neuron_1", "neuron_2")


CEILING = 32.0


def gathered_by_axis(value, axes, dim):
    if not axes:
        return value
    nearer = lax.all_gather(value, axes[-1], axis=dim, tiled=True)
    return gathered_by_axis(nearer, axes[:-1], dim)


def local(images, tile_weights, tile_blocks, tile_count, bias):
    devices = lax.axis_size(NEURON)
    layer_total = tile_weights.shape[0]
    slot_total = tile_weights.shape[1]
    block_width = tile_weights.shape[2]
    image_rows, local_width = images.shape
    own_blocks = local_width // block_width
    all_blocks = own_blocks * devices
    capacity = max(2, slot_total // devices)
    slot_ids = jnp.arange(slot_total, dtype=jnp.int32)
    activity = images
    for layer_index in range(layer_total):
        whole_acts = gathered_by_axis(activity, NEURON, 1)
        block_view = whole_acts.reshape(image_rows, all_blocks, block_width)
        row_ids = tile_blocks[layer_index, :, 0]
        col_ids = tile_blocks[layer_index, :, 1]
        usable = slot_ids < tile_count[layer_index, 0]
        picked = jnp.take(block_view, row_ids, axis=1)
        products = jnp.einsum(
            "bsk,skn->sbn", picked, tile_weights[layer_index], preferred_element_type=jnp.float32
        )
        products = jnp.where(usable[:, None, None], products, 0.0)
        owners = col_ids // own_blocks
        local_block = (col_ids % own_blocks).astype(jnp.float32)
        same_owner = (
            (owners[:, None] == owners[None, :])
            & usable[None, :]
            & (slot_ids[None, :] < slot_ids[:, None])
        )
        slot_rank = jnp.sum(same_owner.astype(jnp.int32), axis=1)
        targets = jnp.where(usable, owners * capacity + slot_rank, devices * capacity)
        outgoing = (
            jnp.zeros((devices * capacity, image_rows, block_width), jnp.float32)
            .at[targets]
            .set(products, mode="drop")
        )
        labels = (
            jnp.full((devices * capacity,), -1.0, jnp.float32)
            .at[targets]
            .set(local_block, mode="drop")
        )
        incoming, arrived_ids = (
            lax.all_to_all(outgoing, NEURON, split_axis=0, concat_axis=0, tiled=True),
            lax.all_to_all(labels, NEURON, split_axis=0, concat_axis=0, tiled=True),
        )
        selector = (
            arrived_ids[None, :] == jnp.arange(own_blocks, dtype=jnp.float32)[:, None]
        ).astype(jnp.float32)
        summed = jnp.einsum("or,rbn->obn", selector, incoming, precision=lax.Precision.HIGHEST)
        summed = jnp.transpose(summed, (1, 0, 2)).reshape(image_rows, local_width)
        activity = jnp.clip(summed + bias[layer_index][None, :], 0.0, CEILING).astype(jnp.bfloat16)
    return activity


def solution(mesh):
    split = Mesh(
        mesh.devices.reshape(mesh.shape["batch"], 8, 4, 4),
        ("batch", "neuron_0", "neuron_1", "neuron_2"),
    )
    in_specs = (
        P("batch", NEURON),
        P(None, NEURON, None, None),
        P(None, NEURON, None),
        P(None, NEURON),
        P(None, NEURON),
    )
    out_specs = P("batch", NEURON)
    return jax.shard_map(local, mesh=split, in_specs=in_specs, out_specs=out_specs, check_vma=False)
```

profile of v0, /device:TPU:2, one launch (start us, length us, event | category | flops | bytes accessed | tf_op | source)
XLA Modules:
  0.0 307.3 jit_solution(2130739490381186020)
XLA Ops:
  6.5 0.0 all-gather.3.cloned.1.call-start
  6.5 12.1 %all_gather.18 = bf16[16,2048]{1,0:T(8,128)(2,1)S(1)} all-gather(bf16[16,512]{1,0:T(8,128)(2,1)} %param.7), channel_id=1, replica_groups=mesh['batch'=2,'neuron_0'=8,'neuron_1'=4,'neuron_2'=4] {'neuron_2'}, dimensions={1}, use_global_device_ids=true | all-gather | bytes 81920 | tf_op jit(solution)/shard_map/all_gather | solution.py:16
  18.7 13.5 %all_gather.19 = bf16[16,8192]{1,0:T(8,128)(2,1)} all-gather(bf16[16,2048]{1,0:T(8,128)(2,1)S(1)} %all_gather.18), channel_id=1, replica_groups=mesh['batch'=2,'neuron_0'=8,'neuron_1'=4,'neuron_2'=4] {'neuron_1'}, dimensions={1}, use_global_device_ids=true | all-gather | bytes 327680 | tf_op jit(solution)/shard_map/all_gather | solution.py:16
  32.2 0.0 all-gather.3.cloned.1.call-update
  32.2 1.3 fusion.47
  33.5 0.6 iota_compare_fusion.3
  34.2 0.6 iota_compare_fusion.4
  34.7 0.7 fusion.37
  35.4 0.7 fusion.36
  36.1 0.7 and_select_fusion.4
  36.8 0.2 convert_reduce_fusion
  37.0 1.9 fusion.43
  38.9 1.0 scatter_custom_fusion.1
  39.9 0.8 all_to_all.20
  40.7 14.4 %all-to-all-start.1 = ((f32[128,2,1]{1,2,0:T(1,128)}), f32[128,2,1]{1,2,0:T(1,128)S(1)}, u32[]{:S(2)}, u32[]{:S(2)}) async-start(f32[128,2,1]{1,2,0:T(1,128)} %bitcast.13), calls=%async_computation.1 | async-start | bytes 131072 | tf_op jit(solution)/shard_map/all_to_all | solution.py:63
  55.1 0.7 compare_and_fusion
  55.8 20.0 %all-gather.3.cloned.1.call-done = bf16[16,65536]{1,0:T(8,128)(2,1)} async-done(((bf16[16,8192]{1,0:T(8,128)(2,1)}), bf16[16,65536]{1,0:T(8,128)(2,1)}) %all-gather.3.cloned.1.call-update) | async-done | bytes 2097168 | tf_op jit(solution)/shard_map/all_gather | solution.py:16
  75.8 2.0 copy_bitcast_fusion.1
  77.7 0.7 gather_fusion
  78.5 3.2 %fusion.10 = f32[128,16,128]{2,1,0:T(8,128)S(1)} fusion(bf16[2,128,128,128]{3,2,1,0:T(8,128)(2,1)} %param.8, bf16[128,16,128]{2,1,0:T(8,128)(2,1)S(1)} %gather_fusion, pred[128]{0:T(512)(128)(4,1)S(1)} %get-tuple-element.16, pred[128]{0:T(512)(128)(4,1)S(1)} %iota_compare_fusion.3), kind=kOutput, calls=%fused_computation.18 | convolution fusion | flops 67633152 | bytes 5767424 | tf_op jit(solution)/shard_map/bsk,skn->sbn/dot_general | solution.py:38
  81.6 1.5 broadcast.296.clone
  83.1 13.7 %scatter_fusion = f32[256,16,128]{2,1,0:T(8,128)} fusion(f32[256,16,128]{2,1,0:T(8,128)} %broadcast.296.clone, s32[128]{0:T(128)S(1)} %get-tuple-element.18, f32[128,16,128]{2,1,0:T(8,128)S(1)} %fusion.10), kind=kCustom, calls=%fused_computation.4 | custom fusion | bytes 3146240 | tf_op jit(solution)/shard_map/scatter | solution.py:54
  96.8 0.0 copy-start
  96.8 0.0 all-to-all-done.1
  96.8 11.1 %all-to-all-start.2 = ((f32[256,16,128]{2,1,0:T(8,128)}), f32[256,16,128]{2,1,0:T(8,128)S(1)}, u32[]{:S(2)}, u32[]{:S(2)}) async-start(f32[256,16,128]{2,1,0:T(8,128)} %scatter_fusion), calls=%async_computation.2 | async-start | bytes 4194304 | tf_op jit(solution)/shard_map/all_to_all | solution.py:62
  108.0 0.0 all-gather.5.cloned.1.call-start
  108.0 0.0 copy-done
  108.0 0.5 broadcast.363
  108.5 0.8 reduce.6
  109.4 0.1 eq.69
  109.5 46.7 %all-to-all-done.2 = f32[256,16,128]{2,1,0:T(8,128)S(1)} async-done(((f32[256,16,128]{2,1,0:T(8,128)}), f32[256,16,128]{2,1,0:T(8,128)S(1)}, u32[]{:S(2)}, u32[]{:S(2)}) %all-to-all-start.2) | async-done | bytes 2097184 | tf_op jit(solution)/shard_map/all_to_all | solution.py:62
  156.2 1.3 fusion.8
  157.5 11.5 %all_gather.21 = bf16[16,2048]{1,0:T(8,128)(2,1)S(1)} all-gather(bf16[16,512]{1,0:T(8,128)(2,1)S(1)} %fusion.29), channel_id=1, replica_groups=mesh['batch'=2,'neuron_0'=8,'neuron_1'=4,'neuron_2'=4] {'neuron_2'}, dimensions={1}, use_global_device_ids=true | all-gather | bytes 81920 | tf_op jit(solution)/shard_map/all_gather | solution.py:16
  169.0 13.0 %all_gather.22 = bf16[16,8192]{1,0:T(8,128)(2,1)} all-gather(bf16[16,2048]{1,0:T(8,128)(2,1)S(1)} %all_gather.21), channel_id=1, replica_groups=mesh['batch'=2,'neuron_0'=8,'neuron_1'=4,'neuron_2'=4] {'neuron_1'}, dimensions={1}, use_global_device_ids=true | all-gather | bytes 327680 | tf_op jit(solution)/shard_map/all_gather | solution.py:16
  182.0 0.0 all-gather.5.cloned.1.call-update
  182.1 1.0 scatter_custom_fusion
  183.0 0.8 all_to_all.18
  183.8 8.2 %all-to-all-start = ((f32[128,2,1]{1,2,0:T(1,128)}), f32[128,2,1]{1,2,0:T(1,128)S(1)}, u32[]{:S(2)}, u32[]{:S(2)}) async-start(f32[128,2,1]{1,2,0:T(1,128)} %bitcast.5), calls=%async_computation | async-start | bytes 131072 | tf_op jit(solution)/shard_map/all_to_all | solution.py:63
  192.0 27.2 %all-gather.5.cloned.1.call-done = bf16[16,65536]{1,0:T(8,128)(2,1)} async-done(((bf16[16,8192]{1,0:T(8,128)(2,1)}), bf16[16,65536]{1,0:T(8,128)(2,1)}) %all-gather.5.cloned.1.call-update) | async-done | bytes 2097168 | tf_op jit(solution)/shard_map/all_gather | solution.py:16
  219.2 2.0 copy_bitcast_fusion
  221.2 0.7 gather_fusion.1
  221.9 3.2 %fusion.13 = f32[128,16,128]{2,1,0:T(8,128)S(1)} fusion(bf16[2,128,128,128]{3,2,1,0:T(8,128)(2,1)} %param.8, bf16[128,16,128]{2,1,0:T(8,128)(2,1)S(1)} %gather_fusion.1, pred[128]{0:T(512)(128)(4,1)S(1)} %get-tuple-element.8, pred[128]{0:T(512)(128)(4,1)S(1)} %iota_compare_fusion.4), kind=kOutput, calls=%fused_computation.19 | convolution fusion | flops 67633152 | bytes 5767424 | tf_op jit(solution)/shard_map/bsk,skn->sbn/dot_general | solution.py:38
  225.1 1.5 broadcast.296
  226.5 13.6 %scatter_fusion.1 = f32[256,16,128]{2,1,0:T(8,128)} fusion(f32[256,16,128]{2,1,0:T(8,128)} %broadcast.296, s32[128]{0:T(128)S(1)} %get-tuple-element.19, f32[128,16,128]{2,1,0:T(8,128)S(1)} %fusion.13), kind=kCustom, calls=%fused_computation.5 | custom fusion | bytes 3146240 | tf_op jit(solution)/shard_map/scatter | solution.py:54
  240.1 0.0 all-to-all-done
  240.1 11.3 %all-to-all-start.3 = ((f32[256,16,128]{2,1,0:T(8,128)}), f32[256,16,128]{2,1,0:T(8,128)S(1)}, u32[]{:S(2)}, u32[]{:S(2)}) async-start(f32[256,16,128]{2,1,0:T(8,128)} %scatter_fusion.1), calls=%async_computation.3 | async-start | bytes 4194304 | tf_op jit(solution)/shard_map/all_to_all | solution.py:62
  251.4 0.8 reduce.7
  252.3 0.1 eq.62
  252.4 46.1 %all-to-all-done.3 = f32[256,16,128]{2,1,0:T(8,128)S(1)} async-done(((f32[256,16,128]{2,1,0:T(8,128)}), f32[256,16,128]{2,1,0:T(8,128)S(1)}, u32[]{:S(2)}, u32[]{:S(2)}) %all-to-all-start.3) | async-done | bytes 2097184 | tf_op jit(solution)/shard_map/all_to_all | solution.py:62
  298.5 1.3 fusion.6
  299.8 0.6 fusion.27
  (4 shorter events, 0.0 us)
Async XLA Ops:
  6.5 69.3 %all-gather.3.cloned.1.call-start = ((), (), s32[]{:S(2)}) async-start(), calls=%async_computation.4 | async-start | bytes 2359296 | tf_op jit(solution)/shard_map/all_gather | solution.py:16
  40.7 56.1 %all-to-all-start.1 = ((f32[128,2,1]{1,2,0:T(1,128)}), f32[128,2,1]{1,2,0:T(1,128)S(1)}, u32[]{:S(2)}, u32[]{:S(2)}) async-start(f32[128,2,1]{1,2,0:T(1,128)} %bitcast.13), calls=%async_computation.1 | async-start | bytes 131072 | tf_op jit(solution)/shard_map/all_to_all | solution.py:63
  96.8 11.2 %copy-start = (f32[2,512]{1,0:T(2,128)S(1)}, f32[2,512]{1,0:T(2,128)}, u32[]{:S(2)}) copy-start(f32[2,512]{1,0:T(2,128)} %param.11) | copy-start | bytes 12292
  96.8 59.4 %all-to-all-start.2 = ((f32[256,16,128]{2,1,0:T(8,128)}), f32[256,16,128]{2,1,0:T(8,128)S(1)}, u32[]{:S(2)}, u32[]{:S(2)}) async-start(f32[256,16,128]{2,1,0:T(8,128)} %scatter_fusion), calls=%async_computation.2 | async-start | bytes 4194304 | tf_op jit(solution)/shard_map/all_to_all | solution.py:62
  108.0 111.3 %all-gather.5.cloned.1.call-start = ((), (), s32[]{:S(2)}) async-start(), calls=%async_computation.5 | async-start | bytes 2359296 | tf_op jit(solution)/shard_map/all_gather | solution.py:16
  183.8 56.3 %all-to-all-start = ((f32[128,2,1]{1,2,0:T(1,128)}), f32[128,2,1]{1,2,0:T(1,128)S(1)}, u32[]{:S(2)}, u32[]{:S(2)}) async-start(f32[128,2,1]{1,2,0:T(1,128)} %bitcast.5), calls=%async_computation | async-start | bytes 131072 | tf_op jit(solution)/shard_map/all_to_all | solution.py:63
  240.1 58.4 %all-to-all-start.3 = ((f32[256,16,128]{2,1,0:T(8,128)}), f32[256,16,128]{2,1,0:T(8,128)S(1)}, u32[]{:S(2)}, u32[]{:S(2)}) async-start(f32[256,16,128]{2,1,0:T(8,128)} %scatter_fusion.1), calls=%async_computation.3 | async-start | bytes 4194304 | tf_op jit(solution)/shard_map/all_to_all | solution.py:62
Sparse Core Ops, SparseCore 0:
  32.3 43.4 all-gather.2
  182.2 36.9 all-gather.4
where the time goes:
time: 310 us; the launch traced here: 307 us
  waiting for transfers between devices  140 us (45%)
  blocking collectives  50.1 us (16%)
  starting transfers between devices  45.1 us (15%)
  local copies, waits for them, and re-layouts  41.1 us (13%)
  between operations  13.6 us (4%)
  matrix products  9 us (3%)
  other arithmetic  8.36 us (3%)
    all_to_all x2, waiting for transfers between devices, local(): lax.all_to_all(outgoing, NEURON, split_axis=0, concat_axis=0, tiled=True)  92.7 us
    all_gather x4, blocking collectives, gathered_by_axis(): nearer = lax.all_gather(value, axes[-1], axis=dim, tiled=True)  50.1 us
    all_gather x2, waiting for transfers between devices, gathered_by_axis(): nearer = lax.all_gather(value, axes[-1], axis=dim, tiled=True)  47.2 us
    scatter x2, local copies, waits for them, and re-layouts, local(): outgoing = jnp.zeros((devices * capacity, image_rows, block_width), jnp.f...  27.3 us
    all_to_all x2, starting transfers between devices, local(): lax.all_to_all(labels, NEURON, split_axis=0, concat_axis=0, tiled=True)  22.6 us
    all_to_all x2, starting transfers between devices, local(): lax.all_to_all(outgoing, NEURON, split_axis=0, concat_axis=0, tiled=True)  22.5 us
    dot_general x2, matrix products, local(): jnp.einsum('bsk,skn->sbn', picked, tile_weights[layer_index], preferred_e...  6.35 us
  transfers between devices with their start and end apart: 6, of which 4 were waited for; matrix products, arithmetic and copies ran while one was open for 17% of the time, Pallas kernels for 0%

commit v1 on v0

v1 whole, which is shorter than its diff:
```python
import functools

import jax
import jax.numpy as jnp
from jax import lax
from jax.experimental import pallas as pl
from jax.experimental.pallas import tpu as pltpu
from jax.sharding import Mesh
from jax.sharding import PartitionSpec as P

NEURON = ("neuron_0", "neuron_1", "neuron_2")
PLANE = ("neuron_1", "neuron_2")
CEILING = 32.0
WIRE = jnp.float16

SMEM = functools.partial(pl.BlockSpec, memory_space=pltpu.SMEM)
VMEM = functools.partial(pl.BlockSpec, memory_space=pltpu.VMEM)
ANY = functools.partial(pl.BlockSpec, memory_space=pl.ANY)


def label_kernel(planes, heights, own, slots, blocks_ref, count_ref, label_ref, target_ref, fill_ref):
    room = slots // planes * 2
    for layer in range(blocks_ref.shape[0]):
        for p in range(planes):
            fill_ref[p] = 0
        for t in range(planes * room):
            label_ref[t // room, layer * room + t % room] = heights * own

        def place(s, carry):
            col = blocks_ref[layer, 1, s]
            owner = col // own
            p = owner % planes
            k = fill_ref[p]

            @pl.when(s < count_ref[layer, 0])
            def _():
                fill_ref[p] = k + 1
                label_ref[p, layer * room + k] = (owner // planes) * own + col % own
                target_ref[layer, s] = p * room + k

            return carry

        lax.fori_loop(0, slots, place, 0)


def product_kernel(layer, chunks, sure, blocks_ref, target_ref, count_ref, acts_ref, weights_ref, out_ref, held_ref, sems):
    planes, heights = acts_ref.shape[0], acts_ref.shape[1]
    slots, width = held_ref.shape[0], held_ref.shape[1]
    per = slots // chunks
    own = acts_ref.shape[3] // width
    copies = [
        pltpu.make_async_copy(
            weights_ref.at[layer, pl.ds(c * per, per)], held_ref.at[pl.ds(c * per, per)], sems.at[c]
        )
        for c in range(chunks)
    ]
    for copy in copies:
        copy.start()
    out_ref[...] = jnp.zeros_like(out_ref)

    def one(s):
        row = blocks_ref[layer, 0, s]
        owner = row // own
        lane = pl.multiple_of((row % own) * width, width)
        picked = acts_ref[owner % planes, owner // planes, :, pl.ds(lane, width)]
        product = jnp.dot(picked, held_ref[s], preferred_element_type=jnp.float32)
        out_ref[target_ref[layer, s]] = product.astype(out_ref.dtype)

    for c in range(chunks):
        copies[c].wait()
        for i in range(per):
            s = c * per + i
            if s < sure:
                one(s)
            else:
                pl.when(s < count_ref[layer, 0])(functools.partial(one, s))


def last_kernel(layer, got_ref, bias_ref, out_ref):
    heights, own, rows, width = got_ref.shape
    for b in range(own):
        total = got_ref[0, b]
        for z in range(1, heights):
            total += got_ref[z, b]
        total += bias_ref[layer : layer + 1, b * width : (b + 1) * width]
        done = jnp.clip(total, 0.0, CEILING).astype(out_ref.dtype)
        for z in range(out_ref.shape[0]):
            out_ref[z, :, b * width : (b + 1) * width] = done


def exchanged(value, axes):
    return lax.all_to_all(value, axes, split_axis=0, concat_axis=0, tiled=True)


def local(images, tile_weights, tile_blocks, tile_count, bias):
    layers, slots, width, _ = tile_weights.shape
    rows, local_width = images.shape
    own = local_width // width
    planes = lax.axis_size(PLANE)
    heights = lax.axis_size(NEURON[0])
    room = slots // planes * 2
    chunks = 8
    sure = slots - slots // 4
    blocks = tile_blocks.transpose(0, 2, 1)

    labels, targets = pl.pallas_call(
        functools.partial(label_kernel, planes, heights, own, slots),
        out_shape=(
            jax.ShapeDtypeStruct((planes, layers * room), jnp.int32),
            jax.ShapeDtypeStruct((layers, slots), jnp.int32),
        ),
        in_specs=[SMEM(), SMEM()],
        out_specs=(SMEM(), SMEM()),
        scratch_shapes=[pltpu.SMEM((planes,), jnp.int32)],
        name="labels",
    )(blocks, tile_count)
    labels = exchanged(labels, PLANE)
    dense = jnp.arange(heights * own, dtype=jnp.int32)[:, None]

    copies = jnp.broadcast_to(images[None], (heights, rows, local_width))
    for layer in range(layers):
        column = exchanged(copies, NEURON[0])
        spread = jnp.broadcast_to(column[None], (planes, heights, rows, local_width))
        acts = exchanged(spread, PLANE)
        outgoing = pl.pallas_call(
            functools.partial(product_kernel, layer, chunks, sure),
            out_shape=jax.ShapeDtypeStruct((planes * room, rows, width), jnp.float32),
            in_specs=[SMEM(), SMEM(), SMEM(), VMEM(), ANY()],
            out_specs=VMEM(),
            scratch_shapes=[
                pltpu.VMEM((slots, width, width), jnp.bfloat16),
                pltpu.SemaphoreType.DMA((chunks,)),
            ],
            name="products",
        )(blocks, targets, tile_count, acts.reshape(planes, heights, rows, local_width), tile_weights)
        got = exchanged(outgoing.astype(WIRE), PLANE)
        chosen = (labels[:, layer * room : (layer + 1) * room].reshape(1, -1) == dense).astype(jnp.float32)
        middle = jnp.einsum(
            "or,rbn->obn", chosen, got.astype(jnp.float32), precision=lax.Precision.HIGH
        )
        ended = exchanged(middle.astype(WIRE), NEURON[0]).astype(jnp.float32)
        out_copies = heights if layer + 1 < layers else 1
        copies = pl.pallas_call(
            functools.partial(last_kernel, layer),
            out_shape=jax.ShapeDtypeStruct((out_copies, rows, local_width), jnp.bfloat16),
            in_specs=[VMEM(), VMEM()],
            out_specs=VMEM(),
            name="last",
        )(ended.reshape(heights, own, rows, width), bias)
    return copies[0]


def solution(mesh):
    split = Mesh(
        mesh.devices.reshape(mesh.shape["batch"], 8, 4, 4),
        ("batch", "neuron_0", "neuron_1", "neuron_2"),
    )
    in_specs = (
        P("batch", NEURON),
        P(None, NEURON, None, None),
        P(None, NEURON, None),
        P(None, NEURON),
        P(None, NEURON),
    )
    out_specs = P("batch", NEURON)
    return jax.shard_map(local, mesh=split, in_specs=in_specs, out_specs=out_specs, check_vma=False)
```

time: 310 us -> 195 us (0.63)
  waiting for transfers between devices: 140 us -> 44 us
  local copies, waits for them, and re-layouts: 41.1 us -> 3.6 us
  blocking collectives: 50.1 us -> 82.9 us
  Pallas kernels: 0 us -> 27.2 us
  starting transfers between devices: 45.1 us -> 28.7 us
  between operations: 13.6 us -> 0.09 us
  matrix products: 9 us -> 1.38 us
    all_to_all x0 -> x5, blocking collectives: none -> 82.9 us  [exchanged(): return lax.all_to_all(value, axes, split_axis=0, concat_axis=0, tiled=True)]
    all_gather x4 -> x0, blocking collectives: 50.1 us -> none  [gathered_by_axis(): nearer = lax.all_gather(value, axes[-1], axis=dim, tiled=True)]
    all_to_all x4, waiting for transfers between devices: 92.8 us -> 44 us  [exchanged(): return lax.all_to_all(value, axes, split_axis=0, concat_axis=0, tiled=True)]
    all_gather x2 -> x0, waiting for transfers between devices: 47.2 us -> none  [gathered_by_axis(): nearer = lax.all_gather(value, axes[-1], axis=dim, tiled=True)]
    scatter x4 -> x0, local copies, waits for them, and re-layouts: 29.2 us -> none  [the longest x2 27.3 us: local(): outgoing = jnp.zeros((devices * capacity, image_rows, block_width), jnp.f...]
    pallas_call x0 -> x5, Pallas kernels: none -> 27.2 us  [the longest x2 15.7 us: local(): pl.pallas_call(functools.partial(product_kernel, layer, chunks, sure), ou...]
    all_to_all x4, starting transfers between devices: 45.1 us -> 28.7 us  [exchanged(): return lax.all_to_all(value, axes, split_axis=0, concat_axis=0, tiled=True)]
    dot_general x4 -> x2, matrix products: 9 us -> 1.38 us  [local(): jnp.einsum('or,rbn->obn', chosen, got.astype(jnp.float32), precision=lax....]
  transfers between devices with their start and end apart: 6 -> 4, of which waited for: 4 -> 3; matrix products, arithmetic and copies ran while one was open for 17% -> 2% of each run, Pallas kernels for 0% -> 8%
where the time goes in v1:
time: 195 us
  blocking collectives  82.9 us (43%)
  waiting for transfers between devices  44 us (23%)
  starting transfers between devices  28.7 us (15%)
  Pallas kernels  27.2 us (14%)
  other arithmetic  6.89 us (4%)
  local copies, waits for them, and re-layouts  3.6 us (2%)
    all_to_all x5, blocking collectives, exchanged(): return lax.all_to_all(value, axes, split_axis=0, concat_axis=0, tiled=True)  82.9 us
    all_to_all x4, waiting for transfers between devices, exchanged(): return lax.all_to_all(value, axes, split_axis=0, concat_axis=0, tiled=True)  44 us
    all_to_all x4, starting transfers between devices, exchanged(): return lax.all_to_all(value, axes, split_axis=0, concat_axis=0, tiled=True)  28.7 us
    pallas_call x2, Pallas kernels, local(): pl.pallas_call(functools.partial(product_kernel, layer, chunks, sure), ou...  15.7 us
    pallas_call x1, Pallas kernels, local(): pl.pallas_call(functools.partial(label_kernel, planes, heights, own, slot...  8.24 us
    convert_element_type x2, other arithmetic, local(): got = exchanged(outgoing.astype(WIRE), PLANE)  5.43 us
  transfers between devices with their start and end apart: 4, of which 3 were waited for; matrix products, arithmetic and copies ran while one was open for 2% of the time, Pallas kernels for 8%

profile of v1, /device:TPU:2, one launch (start us, length us, event | category | flops | bytes accessed | tf_op | source)
XLA Modules:
  0.0 194.7 jit_solution(7021133058257598827)
XLA Ops:
  0.0 0.7 broadcast_in_dim.6
  0.7 17.4 %all_to_all.52 = bf16[8,16,512]{2,1,0:T(8,128)(2,1)S(1)} all-to-all(bf16[8,16,512]{2,1,0:T(8,128)(2,1)S(1)} %broadcast_in_dim.6), channel_id=1, replica_groups=mesh['batch'=2,'neuron_0'=8,'neuron_1'=4,'neuron_2'=4] {'neuron_0'}, dimensions={0} | all-to-all | bytes 262144 | tf_op jit(solution)/shard_map/all_to_all | solution.py:92
  18.1 1.6 broadcast_in_dim.7
  19.7 0.0 copy-start.1
  19.7 7.6 %all-to-all-start.2 = ((bf16[16,8,16,512]{3,2,1,0:T(8,128)(2,1)}), bf16[16,8,16,512]{3,2,1,0:T(8,128)(2,1)S(1)}, u32[]{:S(2)}, u32[]{:S(2)}) async-start(bf16[16,8,16,512]{3,2,1,0:T(8,128)(2,1)} %broadcast_in_dim.7), calls=%async_computation.2 | async-start | bytes 4194304 | tf_op jit(solution)/shard_map/all_to_all | solution.py:92
  27.3 0.0 copy-done.1
  27.3 0.7 copy.13.count_ref
  28.0 8.2 %labels.1 = (s32[16,32]{1,0:T(8,128)}, s32[2,128]{1,0:T(2,128)}) custom-call(s32[2,2,128]{2,1,0:T(2,128)} %bitcast.19, s32[2,1]{1,0:T(2,128)} %copy.13.count_ref), custom_call_target="tpu_custom_call" | custom-call | tf_op jit(solution)/shard_map/labels/pallas_call | solution.py:106
  36.2 16.6 %all-to-all-done.2.acts_ref = bf16[16,8,16,512]{3,2,1,0:T(8,128)(2,1)S(1)} async-done(((bf16[16,8,16,512]{3,2,1,0:T(8,128)(2,1)}), bf16[16,8,16,512]{3,2,1,0:T(8,128)(2,1)S(1)}, u32[]{:S(2)}, u32[]{:S(2)}) %all-to-all-start.2) | async-done | bytes 2097184 | tf_op jit(solution)/shard_map/all_to_all | solution.py:92
  52.8 0.0 copy-start
  52.8 6.6 %all-to-all-start = ((s32[16,1,32]{2,1,0:T(1,128)}), s32[16,1,32]{2,1,0:T(1,128)S(1)}, u32[]{:S(2)}, u32[]{:S(2)}) async-start(s32[16,1,32]{2,1,0:T(1,128)} %bitcast.22), calls=%async_computation | async-start | bytes 16384 | tf_op jit(solution)/shard_map/all_to_all | solution.py:92
  59.4 0.0 copy-done
  59.4 7.4 %products.2 = f32[256,16,128]{2,1,0:T(8,128)} custom-call(s32[2,2,128]{2,1,0:T(2,128)} %bitcast.20, s32[2,128]{1,0:T(2,128)} %get-tuple-element.8.target_ref, s32[2,1]{1,0:T(2,128)} %copy.13.count_ref, bf16[16,8,16,512]{3,2,1,0:T(8,128)(2,1)} %copy-done, bf16[2,128,128,128]{3,2,1,0:T(8,128)(2,1)} %weights_ref.3), custom_call_target="tpu_custom_call" | custom-call | tf_op jit(solution)/shard_map/products/pallas_call | solution.py:125
  66.8 2.7 %convert_element_type.8 = f16[256,16,128]{2,1,0:T(8,128)(2,1)} convert(f32[256,16,128]{2,1,0:T(8,128)} %products.2) | non-fusion elementwise | flops 524288 | bytes 3145728 | tf_op jit(solution)/shard_map/convert_element_type | solution.py:136
  69.5 0.0 all-to-all-done
  69.5 8.1 %all-to-all-start.3 = ((f16[256,16,128]{2,1,0:T(8,128)(2,1)}), f16[256,16,128]{2,1,0:T(8,128)(2,1)S(1)}, u32[]{:S(2)}, u32[]{:S(2)}) async-start(f16[256,16,128]{2,1,0:T(8,128)(2,1)} %convert_element_type.8), calls=%async_computation.3 | async-start | bytes 2097152 | tf_op jit(solution)/shard_map/all_to_all | solution.py:92
  77.6 0.1 fusion.8
  77.7 0.1 eq.34
  77.8 14.8 %all-to-all-done.3 = f16[256,16,128]{2,1,0:T(8,128)(2,1)S(1)} async-done(((f16[256,16,128]{2,1,0:T(8,128)(2,1)}), f16[256,16,128]{2,1,0:T(8,128)(2,1)S(1)}, u32[]{:S(2)}, u32[]{:S(2)}) %all-to-all-start.3) | async-done | bytes 1048608 | tf_op jit(solution)/shard_map/all_to_all | solution.py:92
  92.6 0.7 convolution_convert_fusion.1
  93.3 0.1 copy.17
  93.3 12.9 %all_to_all.53 = f16[32,16,128]{2,1,0:T(8,128)(2,1)S(1)} all-to-all(f16[32,16,128]{2,1,0:T(8,128)(2,1)S(1)} %copy.17), channel_id=1, replica_groups=mesh['batch'=2,'neuron_0'=8,'neuron_1'=4,'neuron_2'=4] {'neuron_0'}, dimensions={0} | all-to-all | bytes 262144 | tf_op jit(solution)/shard_map/all_to_all | solution.py:92
  106.2 0.7 convert.2.got_ref
  107.0 1.6 last.2
  108.6 12.3 %all_to_all.54 = bf16[8,16,512]{2,1,0:T(8,128)(2,1)S(1)} all-to-all(bf16[8,16,512]{2,1,0:T(8,128)(2,1)} %last.2), channel_id=1, replica_groups=mesh['batch'=2,'neuron_0'=8,'neuron_1'=4,'neuron_2'=4] {'neuron_0'}, dimensions={0} | all-to-all | bytes 262144 | tf_op jit(solution)/shard_map/all_to_all | solution.py:92
  120.9 0.2 broadcast_in_dim.8
  121.2 28.9 %all_to_all.55.acts_ref = bf16[16,8,16,512]{3,2,1,0:T(8,128)(2,1)} all-to-all(bf16[16,8,16,512]{3,2,1,0:T(8,128)(2,1)S(1)} %broadcast_in_dim.8), channel_id=1, replica_groups=mesh['batch'=2,'neuron_0'=8,'neuron_1'=4,'neuron_2'=4] {'neuron_1','neur..., dimensions={0} | all-to-all | bytes 4194304 | tf_op jit(solution)/shard_map/all_to_all | solution.py:92
  150.0 8.4 %products.3 = f32[256,16,128]{2,1,0:T(8,128)} custom-call(s32[2,2,128]{2,1,0:T(2,128)} %bitcast.21, s32[2,128]{1,0:T(2,128)} %get-tuple-element.8.target_ref, s32[2,1]{1,0:T(2,128)} %copy.13.count_ref, bf16[16,8,16,512]{3,2,1,0:T(8,128)(2,1)} %all_to_all.55.acts_ref, bf16[2,128,128,128]{3,2,1,0:T(8,128)(2,1)} %weights_ref.3), custom_call_target="tpu_custom_call" | custom-call | tf_op jit(solution)/shard_map/products/pallas_call | solution.py:125
  158.4 2.7 %convert_element_type.20 = f16[256,16,128]{2,1,0:T(8,128)(2,1)} convert(f32[256,16,128]{2,1,0:T(8,128)} %products.3) | non-fusion elementwise | flops 524288 | bytes 3145728 | tf_op jit(solution)/shard_map/convert_element_type | solution.py:136
  161.1 6.4 %all-to-all-start.7 = ((f16[256,16,128]{2,1,0:T(8,128)(2,1)}), f16[256,16,128]{2,1,0:T(8,128)(2,1)S(1)}, u32[]{:S(2)}, u32[]{:S(2)}) async-start(f16[256,16,128]{2,1,0:T(8,128)(2,1)} %convert_element_type.20), calls=%async_computation.7 | async-start | bytes 2097152 | tf_op jit(solution)/shard_map/all_to_all | solution.py:92
  167.5 0.1 eq.30
  167.6 12.6 %all-to-all-done.7 = f16[256,16,128]{2,1,0:T(8,128)(2,1)S(1)} async-done(((f16[256,16,128]{2,1,0:T(8,128)(2,1)}), f16[256,16,128]{2,1,0:T(8,128)(2,1)S(1)}, u32[]{:S(2)}, u32[]{:S(2)}) %all-to-all-start.7) | async-done | bytes 1048608 | tf_op jit(solution)/shard_map/all_to_all | solution.py:92
  180.2 0.7 convolution_convert_fusion
  180.9 0.1 copy.20
  181.0 11.5 %all_to_all.56 = f16[32,16,128]{2,1,0:T(8,128)(2,1)S(1)} all-to-all(f16[32,16,128]{2,1,0:T(8,128)(2,1)S(1)} %copy.20), channel_id=1, replica_groups=mesh['batch'=2,'neuron_0'=8,'neuron_1'=4,'neuron_2'=4] {'neuron_0'}, dimensions={0} | all-to-all | bytes 262144 | tf_op jit(solution)/shard_map/all_to_all | solution.py:92
  192.4 0.7 convert.3.got_ref
  193.2 1.6 last.3
Async XLA Ops:
  19.7 7.6 %copy-start.1 = (s32[2,1]{0,1:T(1,128)S(1)}, s32[2,1]{0,1:T(1,128)}, u32[]{:S(2)}) copy-start(s32[2,1]{0,1:T(1,128)} %param.8) | copy-start | bytes 28
  19.7 33.1 %all-to-all-start.2 = ((bf16[16,8,16,512]{3,2,1,0:T(8,128)(2,1)}), bf16[16,8,16,512]{3,2,1,0:T(8,128)(2,1)S(1)}, u32[]{:S(2)}, u32[]{:S(2)}) async-start(bf16[16,8,16,512]{3,2,1,0:T(8,128)(2,1)} %broadcast_in_dim.7), calls=%async_computation.2 | async-start | bytes 4194304 | tf_op jit(solution)/shard_map/all_to_all | solution.py:92
  52.8 6.6 %copy-start = (bf16[16,8,16,512]{3,2,1,0:T(8,128)(2,1)}, bf16[16,8,16,512]{3,2,1,0:T(8,128)(2,1)S(1)}, u32[]{:S(2)}) copy-start(bf16[16,8,16,512]{3,2,1,0:T(8,128)(2,1)S(1)} %all-to-all-done.2.acts_ref) | copy-start | bytes 6291460
  52.8 16.7 %all-to-all-start = ((s32[16,1,32]{2,1,0:T(1,128)}), s32[16,1,32]{2,1,0:T(1,128)S(1)}, u32[]{:S(2)}, u32[]{:S(2)}) async-start(s32[16,1,32]{2,1,0:T(1,128)} %bitcast.22), calls=%async_computation | async-start | bytes 16384 | tf_op jit(solution)/shard_map/all_to_all | solution.py:92
  69.5 23.1 %all-to-all-start.3 = ((f16[256,16,128]{2,1,0:T(8,128)(2,1)}), f16[256,16,128]{2,1,0:T(8,128)(2,1)S(1)}, u32[]{:S(2)}, u32[]{:S(2)}) async-start(f16[256,16,128]{2,1,0:T(8,128)(2,1)} %convert_element_type.8), calls=%async_computation.3 | async-start | bytes 2097152 | tf_op jit(solution)/shard_map/all_to_all | solution.py:92
  161.1 19.1 %all-to-all-start.7 = ((f16[256,16,128]{2,1,0:T(8,128)(2,1)}), f16[256,16,128]{2,1,0:T(8,128)(2,1)S(1)}, u32[]{:S(2)}, u32[]{:S(2)}) async-start(f16[256,16,128]{2,1,0:T(8,128)(2,1)} %convert_element_type.20), calls=%async_computation.7 | async-start | bytes 2097152 | tf_op jit(solution)/shard_map/all_to_all | solution.py:92

commit v2 on v0

v2 whole, which is shorter than its diff:
```python
import jax
import jax.numpy as jnp
from jax import lax
from jax.sharding import Mesh
from jax.sharding import PartitionSpec as P

NEURON = ("neuron_0", "neuron_1", "neuron_2")
HEIGHT = NEURON[0]
PLANE = NEURON[1:]
CEILING = 32.0
WIRE = jnp.float16


def exchanged(value, axes):
    return lax.all_to_all(value, axes, split_axis=0, concat_axis=0, tiled=True)


def local(images, tile_weights, tile_blocks, tile_count, bias):
    layers, slots, width, _ = tile_weights.shape
    rows, local_width = images.shape
    own = local_width // width
    heights = lax.axis_size(HEIGHT)
    planes = lax.axis_size(PLANE)
    each = rows // planes
    held = planes * own
    every = heights * held
    block_ids = jnp.arange(every, dtype=jnp.int32)

    live = jnp.arange(slots, dtype=jnp.int32)[None, :] < tile_count
    routes = jnp.where(live[:, None, :], tile_blocks.transpose(0, 2, 1), -1)
    facts = jnp.concatenate(
        [routes.reshape(layers * 2, slots).astype(jnp.float32), bias.reshape(layers * own, width)], axis=0
    )
    opening = jnp.concatenate(
        [
            images.reshape(planes, each * own, width).astype(jnp.float32),
            jnp.broadcast_to(facts[None], (planes,) + facts.shape),
        ],
        axis=1,
    )
    opened = exchanged(opening, PLANE)
    state = opened[:, :own].reshape(held, width).astype(jnp.bfloat16)
    routes = opened[:, own : own + layers * 2].astype(jnp.int32)
    biases = opened[:, own + layers * 2 :]

    for layer in range(layers):
        spread = jnp.broadcast_to(state[None], (heights, held, width)).reshape(every, width)
        acts = exchanged(spread, HEIGHT)
        from_rows = (routes[:, layer * 2].reshape(-1)[:, None] == block_ids[None, :]).astype(jnp.bfloat16)
        wanted = jnp.dot(from_rows, acts, preferred_element_type=jnp.float32).astype(jnp.bfloat16)
        picked = exchanged(wanted.reshape(planes, slots, width), PLANE)
        products = jnp.einsum("isk,skn->isn", picked, tile_weights[layer], preferred_element_type=jnp.float32)
        returned = exchanged(products.astype(WIRE), PLANE)
        to_cols = (block_ids[:, None] == routes[:, layer * 2 + 1].reshape(-1)[None, :]).astype(jnp.float32)
        partial = jnp.dot(
            to_cols, returned.reshape(planes * slots, width).astype(jnp.float32), precision=lax.Precision.HIGH
        )
        ended = exchanged(partial.astype(WIRE), HEIGHT).reshape(heights, held, width)
        summed = jnp.sum(ended.astype(jnp.float32), axis=0)
        summed += biases[:, layer * own : (layer + 1) * own].reshape(held, width)
        state = jnp.clip(summed, 0.0, CEILING).astype(jnp.bfloat16)
    return exchanged(state.reshape(planes, own, width), PLANE).reshape(rows, local_width)


def solution(mesh):
    split = Mesh(
        mesh.devices.reshape(mesh.shape["batch"], 8, 4, 4),
        ("batch", "neuron_0", "neuron_1", "neuron_2"),
    )
    in_specs = (
        P("batch", NEURON),
        P(None, NEURON, None, None),
        P(None, NEURON, None),
        P(None, NEURON),
        P(None, NEURON),
    )
    out_specs = P("batch", NEURON)
    return jax.shard_map(local, mesh=split, in_specs=in_specs, out_specs=out_specs, check_vma=False)
```

time: 310 us -> 144 us (0.46)
  waiting for transfers between devices: 140 us -> 9.03 us
  blocking collectives: 50.1 us -> 111 us
  local copies, waits for them, and re-layouts: 41.1 us -> 3.15 us
  starting transfers between devices: 45.1 us -> 8.47 us
  between operations: 13.6 us -> 0.11 us
  other arithmetic: 8.36 us -> 1.53 us
    all_to_all x0 -> x9, blocking collectives: none -> 111 us  [exchanged(): return lax.all_to_all(value, axes, split_axis=0, concat_axis=0, tiled=True)]
    all_to_all x4 -> x1, waiting for transfers between devices: 92.8 us -> 9.03 us  [exchanged(): return lax.all_to_all(value, axes, split_axis=0, concat_axis=0, tiled=True)]
    all_gather x4 -> x0, blocking collectives: 50.1 us -> none  [gathered_by_axis(): nearer = lax.all_gather(value, axes[-1], axis=dim, tiled=True)]
    all_gather x2 -> x0, waiting for transfers between devices: 47.2 us -> none  [gathered_by_axis(): nearer = lax.all_gather(value, axes[-1], axis=dim, tiled=True)]
    all_to_all x4 -> x1, starting transfers between devices: 45.1 us -> 8.47 us  [exchanged(): return lax.all_to_all(value, axes, split_axis=0, concat_axis=0, tiled=True)]
    scatter x4 -> x0, local copies, waits for them, and re-layouts: 29.2 us -> none  [the longest x2 27.3 us: local(): outgoing = jnp.zeros((devices * capacity, image_rows, block_width), jnp.f...]
    reshape x2 -> x1, local copies, waits for them, and re-layouts: 3.9 us -> 0.69 us  [local(): bias.reshape(layers * own, width)]
    dot_general x4 -> x6, matrix products: 9 us -> 9.38 us  [the longest x2 4.8 us: local(): jnp.einsum('isk,skn->isn', picked, tile_weights[layer], preferred_element...]
  transfers between devices with their start and end apart: 6 -> 1, of which waited for: 4 -> 1; matrix products, arithmetic and copies ran while one was open for 17% -> 0% of each run, Pallas kernels for 0% -> 0%
where the time goes in v2:
time: 144 us; the launch traced here: 143 us
  blocking collectives  111 us (77%)
  matrix products  9.38 us (7%)
  waiting for transfers between devices  9.03 us (6%)
  starting transfers between devices  8.47 us (6%)
  local copies, waits for them, and re-layouts  3.15 us (2%)
  other arithmetic  1.53 us (1%)
    all_to_all x9, blocking collectives, exchanged(): return lax.all_to_all(value, axes, split_axis=0, concat_axis=0, tiled=True)  111 us
    all_to_all x1, waiting for transfers between devices, exchanged(): return lax.all_to_all(value, axes, split_axis=0, concat_axis=0, tiled=True)  9.03 us
    all_to_all x1, starting transfers between devices, exchanged(): return lax.all_to_all(value, axes, split_axis=0, concat_axis=0, tiled=True)  8.47 us
    dot_general x2, matrix products, local(): jnp.einsum('isk,skn->isn', picked, tile_weights[layer], preferred_element...  4.8 us
  transfers between devices with their start and end apart: 1, of which 1 were waited for; matrix products, arithmetic and copies ran while one was open for 0% of the time, Pallas kernels for 0%

profile of v2, /device:TPU:2, one launch (start us, length us, event | category | flops | bytes accessed | tf_op | source)
XLA Modules:
  0.0 143.1 jit_solution(15545241784219725597)
XLA Ops:
  0.0 0.7 iota_compare_fusion.16
  0.7 0.7 reshape.84
  1.4 0.7 reshape.91
  2.2 0.7 select_convert_fusion
  2.9 13.9 %all_to_all.66 = f32[16,16,128]{2,1,0:T(8,128)S(1)} all-to-all(f32[16,16,128]{2,1,0:T(8,128)S(1)} %pad_maximum_fusion), channel_id=1, replica_groups=mesh['batch'=2,'neuron_0'=8,'neuron_1'=4,'neuron_2'=4] {'neuron_1','neur..., dimensions={0} | all-to-all | bytes 262144 | tf_op jit(solution)/shard_map/all_to_all | solution.py:15
  16.8 0.7 broadcast_in_dim.21
  17.5 8.5 %all-to-all-start.1 = ((bf16[8,64,128]{2,1,0:T(8,128)(2,1)}), bf16[8,64,128]{2,1,0:T(8,128)(2,1)S(1)}, u32[]{:S(2)}, u32[]{:S(2)}) async-start(bf16[8,64,128]{2,1,0:T(8,128)(2,1)} %broadcast_in_dim.21), calls=%async_computation.1 | async-start | bytes 262144 | tf_op jit(solution)/shard_map/all_to_all | solution.py:15
  26.0 9.0 %all-to-all-done.1 = bf16[8,64,128]{2,1,0:T(8,128)(2,1)S(1)} async-done(((bf16[8,64,128]{2,1,0:T(8,128)(2,1)}), bf16[8,64,128]{2,1,0:T(8,128)(2,1)S(1)}, u32[]{:S(2)}, u32[]{:S(2)}) %all-to-all-start.1) | async-done | bytes 131104 | tf_op jit(solution)/shard_map/all_to_all | solution.py:15
  35.0 0.0 slice-start
  35.0 1.0 fusion.10
  36.1 13.3 %all_to_all.67 = bf16[16,128,128]{2,1,0:T(8,128)(2,1)S(1)} all-to-all(bf16[16,128,128]{2,1,0:T(8,128)(2,1)S(1)} %bitcast.48), channel_id=1, replica_groups=mesh['batch'=2,'neuron_0'=8,'neuron_1'=4,'neuron_2'=4] {'neuron_1','neur..., dimensions={0} | all-to-all | bytes 1048576 | tf_op jit(solution)/shard_map/all_to_all | solution.py:15
  49.4 0.0 slice-start.1
  49.4 3.6 %fusion.25 = f16[16,128,128]{2,0,1:T(8,128)(2,1)S(1)} fusion(bf16[2,128,128,128]{3,2,1,0:T(8,128)(2,1)} %param.6, bf16[16,128,128]{2,1,0:T(8,128)(2,1)S(1)} %all_to_all.67), kind=kOutput, calls=%fused_computation.23 | convolution fusion | flops 67371008 | bytes 5242880 | tf_op jit(solution)/shard_map/isk,skn->isn/dot_general | solution.py:52
  53.0 0.2 copy.13
  53.2 13.1 %all_to_all.68 = f16[16,128,128]{2,1,0:T(8,128)(2,1)S(1)} all-to-all(f16[16,128,128]{2,1,0:T(8,128)(2,1)S(1)} %copy.13), channel_id=1, replica_groups=mesh['batch'=2,'neuron_0'=8,'neuron_1'=4,'neuron_2'=4] {'neuron_1','neur..., dimensions={0} | all-to-all | bytes 1048576 | tf_op jit(solution)/shard_map/all_to_all | solution.py:15
  66.3 1.3 fusion.28
  67.6 11.5 %all_to_all.69 = f16[8,64,128]{2,1,0:T(8,128)(2,1)S(1)} all-to-all(f16[8,64,128]{2,1,0:T(8,128)(2,1)S(1)} %bitcast.53), channel_id=1, replica_groups=mesh['batch'=2,'neuron_0'=8,'neuron_1'=4,'neuron_2'=4] {'neuron_0'}, dimensions={0} | all-to-all | bytes 262144 | tf_op jit(solution)/shard_map/all_to_all | solution.py:15
  79.1 11.5 %all_to_all.70 = bf16[8,64,128]{2,1,0:T(8,128)(2,1)S(1)} all-to-all(bf16[8,64,128]{2,1,0:T(8,128)(2,1)S(1)} %broadcast_in_dim.22), channel_id=1, replica_groups=mesh['batch'=2,'neuron_0'=8,'neuron_1'=4,'neuron_2'=4] {'neuron_0'}, dimensions={0} | all-to-all | bytes 262144 | tf_op jit(solution)/shard_map/all_to_all | solution.py:15
  90.6 1.0 fusion.11
  91.6 13.2 %all_to_all.71 = bf16[16,128,128]{2,1,0:T(8,128)(2,1)S(1)} all-to-all(bf16[16,128,128]{2,1,0:T(8,128)(2,1)S(1)} %bitcast.50), channel_id=1, replica_groups=mesh['batch'=2,'neuron_0'=8,'neuron_1'=4,'neuron_2'=4] {'neuron_1','neur..., dimensions={0} | all-to-all | bytes 1048576 | tf_op jit(solution)/shard_map/all_to_all | solution.py:15
  104.8 0.0 slice-done
  104.8 0.0 slice-done.1
  104.8 1.2 fusion.22
  106.0 0.2 copy.15
  106.2 13.0 %all_to_all.72 = f16[16,128,128]{2,1,0:T(8,128)(2,1)S(1)} all-to-all(f16[16,128,128]{2,1,0:T(8,128)(2,1)S(1)} %copy.15), channel_id=1, replica_groups=mesh['batch'=2,'neuron_0'=8,'neuron_1'=4,'neuron_2'=4] {'neuron_1','neur..., dimensions={0} | all-to-all | bytes 1048576 | tf_op jit(solution)/shard_map/all_to_all | solution.py:15
  119.2 1.3 fusion.29
  120.5 11.5 %all_to_all.73 = f16[8,64,128]{2,1,0:T(8,128)(2,1)S(1)} all-to-all(f16[8,64,128]{2,1,0:T(8,128)(2,1)S(1)} %bitcast.55), channel_id=1, replica_groups=mesh['batch'=2,'neuron_0'=8,'neuron_1'=4,'neuron_2'=4] {'neuron_0'}, dimensions={0} | all-to-all | bytes 262144 | tf_op jit(solution)/shard_map/all_to_all | solution.py:15
  132.0 10.5 %all_to_all.74 = bf16[16,4,128]{2,1,0:T(4,128)(2,1)S(1)} all-to-all(bf16[16,4,128]{2,1,0:T(4,128)(2,1)S(1)} %fusion.33), channel_id=1, replica_groups=mesh['batch'=2,'neuron_0'=8,'neuron_1'=4,'neuron_2'=4] {'neuron_1','neur..., dimensions={0} | all-to-all | bytes 32768 | tf_op jit(solution)/shard_map/all_to_all | solution.py:15
  142.5 0.6 copy.22
  (12 shorter events, 0.2 us)
Async XLA Ops:
  17.5 17.5 %all-to-all-start.1 = ((bf16[8,64,128]{2,1,0:T(8,128)(2,1)}), bf16[8,64,128]{2,1,0:T(8,128)(2,1)S(1)}, u32[]{:S(2)}, u32[]{:S(2)}) async-start(bf16[8,64,128]{2,1,0:T(8,128)(2,1)} %broadcast_in_dim.21), calls=%async_computation.1 | async-start | bytes 262144 | tf_op jit(solution)/shard_map/all_to_all | solution.py:15
  35.0 69.8 %slice-start = ((s8[8388608]{0:T(1024)(128)(4,1)}), s8[4194304]{0:T(1024)(128)(4,1)S(1)}, s32[]{:S(2)}) async-start(s8[8388608]{0:T(1024)(128)(4,1)} %bitcast.45), calls=%async_computation.10 | async-start | bytes 8388608
  49.4 55.4 %slice-start.1 = ((s8[8388608]{0:T(1024)(128)(4,1)}), s8[4194304]{0:T(1024)(128)(4,1)S(1)}, s32[]{:S(2)}) async-start(s8[8388608]{0:T(1024)(128)(4,1)} %bitcast.45), calls=%async_computation.11 | async-start | bytes 8388608

commit v3 on v2

v3 whole, which is shorter than its diff:
```python
import functools

import jax
import jax.numpy as jnp
from jax import lax
from jax.experimental import pallas as pl
from jax.experimental.pallas import tpu as pltpu
from jax.sharding import Mesh
from jax.sharding import PartitionSpec as P

NEURON = ("neuron_0", "neuron_1", "neuron_2")
HEIGHT = NEURON[0]
PLANE = NEURON[1:]
CEILING = 32.0
WIRE = jnp.float16


def exchanged(value, axes):
    return lax.all_to_all(value, axes, split_axis=0, concat_axis=0, tiled=True)


def opening_kernel(count_ref, images_ref, blocks_ref, bias_ref, out_ref):
    layers, sides, slots = blocks_ref.shape
    planes, _, width = out_ref.shape
    own = images_ref.shape[1] // width
    ids = lax.broadcasted_iota(jnp.int32, (1, slots), 1)
    for b in range(own):
        out_ref[:, b, :] = images_ref[:, b * width : (b + 1) * width].astype(jnp.float32)
    at = own
    for layer in range(layers):
        live = ids < count_ref[0, layer]
        for side in range(sides):
            route = jnp.where(live, blocks_ref[layer, side : side + 1, :], -1).astype(jnp.float32)
            out_ref[:, at, :] = jnp.broadcast_to(route, (planes, slots))
            at += 1
    for layer in range(layers):
        for b in range(own):
            part = bias_ref[layer : layer + 1, b * width : (b + 1) * width]
            out_ref[:, at, :] = jnp.broadcast_to(part, (planes, width))
            at += 1


def ranks(match):
    size = match.shape[-1]
    ids = jnp.arange(size, dtype=jnp.int32)
    return jnp.sum((match[..., None, :] & (ids[None, :] < ids[:, None])).astype(jnp.int32), axis=-1)


def local(images, tile_weights, tile_blocks, tile_count, bias):
    layers, slots, width, _ = tile_weights.shape
    rows, local_width = images.shape
    own = local_width // width
    heights = lax.axis_size(HEIGHT)
    planes = lax.axis_size(PLANE)
    me = lax.axis_index(PLANE)
    held = planes * own
    every = heights * held
    room = slots // planes * 2
    block_ids = jnp.arange(every, dtype=jnp.int32)

    opening = pl.pallas_call(
        opening_kernel,
        out_shape=jax.ShapeDtypeStruct((planes, own + layers * 2 + layers * own, width), jnp.float32),
        in_specs=[pl.BlockSpec(memory_space=pltpu.SMEM)] + [pl.BlockSpec(memory_space=pltpu.VMEM)] * 3,
        out_specs=pl.BlockSpec(memory_space=pltpu.VMEM),
        name="opening",
    )(tile_count.T, images, tile_blocks.transpose(0, 2, 1), bias)
    opened = exchanged(opening, PLANE)
    state = opened[:, :own].reshape(held, width).astype(jnp.bfloat16)
    routes = opened[:, own : own + layers * 2].astype(jnp.int32)
    biases = opened[:, own + layers * 2 :]

    own_cols = jnp.where(
        jnp.arange(slots, dtype=jnp.int32) < tile_count[layers - 1, 0], tile_blocks[layers - 1, :, 1], -every
    )
    plane = (own_cols // own) % planes
    same = (plane[:, None] == plane[None, :]) & (own_cols >= 0)[None, :]
    earlier = jnp.arange(slots)[None, :] < jnp.arange(slots)[:, None]
    target = plane * room + jnp.sum((same & earlier).astype(jnp.int32), axis=1)
    target = jnp.where(own_cols >= 0, target, -1)
    cols = routes[:, layers * 2 - 1]
    mine = (cols >= 0) & ((cols // own) % planes == me)
    place = jnp.where(mine, ranks(mine), -1)
    label = jnp.where(mine, (cols // held) * own + cols % own, 0) + 1
    here = place[:, None, :] == jnp.arange(room, dtype=jnp.int32)[None, :, None]
    labels = jnp.sum(jnp.where(here, label[:, None, :], 0), axis=2).reshape(-1)

    packing = (jnp.arange(planes * room, dtype=jnp.int32)[:, None] == target[None, :]).astype(jnp.float32)
    chosen = (jnp.arange(1, heights * own + 1, dtype=jnp.int32)[:, None] == labels[None, :]).astype(jnp.float32)
    last_bias = bias[layers - 1]

    for layer in range(layers):
        spread = jnp.broadcast_to(state[None], (heights, held, width)).reshape(every, width)
        acts = exchanged(spread, HEIGHT)
        if layer == 0:
            acts, packing, chosen, last_bias = lax.optimization_barrier((acts, packing, chosen, last_bias))
        from_rows = (routes[:, layer * 2].reshape(-1)[:, None] == block_ids[None, :]).astype(jnp.bfloat16)
        wanted = jnp.dot(from_rows, acts, preferred_element_type=jnp.float32).astype(jnp.bfloat16)
        picked = exchanged(wanted.reshape(planes, slots, width), PLANE)
        products = jnp.einsum("isk,skn->isn", picked, tile_weights[layer], preferred_element_type=jnp.float32)
        products = products.astype(WIRE)
        if layer + 1 == layers:
            break
        cols = routes[:, layer * 2 + 1]
        returned = exchanged(products, PLANE)
        to_cols = (block_ids[:, None] == cols.reshape(-1)[None, :]).astype(jnp.float32)
        partial = jnp.dot(
            to_cols, returned.reshape(planes * slots, width).astype(jnp.float32), precision=lax.Precision.HIGH
        )
        ended = exchanged(partial.astype(WIRE), HEIGHT).reshape(heights, held, width)
        summed = jnp.sum(ended.astype(jnp.float32), axis=0)
        summed += biases[:, layer * own : (layer + 1) * own].reshape(held, width)
        state = jnp.clip(summed, 0.0, CEILING).astype(jnp.bfloat16)

    packed = jnp.einsum("ts,isn->tin", packing, products.astype(jnp.float32), precision=lax.Precision.HIGH)
    got = exchanged(packed.astype(WIRE), PLANE)
    middle = jnp.einsum("or,rin->oin", chosen, got.astype(jnp.float32), precision=lax.Precision.HIGH)
    ended = exchanged(middle.astype(WIRE), HEIGHT).reshape(heights, own, rows, width)
    summed = jnp.sum(ended.astype(jnp.float32), axis=0).transpose(1, 0, 2).reshape(rows, local_width)
    return jnp.clip(summed + last_bias[None, :], 0.0, CEILING).astype(jnp.bfloat16)


def solution(mesh):
    split = Mesh(
        mesh.devices.reshape(mesh.shape["batch"], 8, 4, 4),
        ("batch", "neuron_0", "neuron_1", "neuron_2"),
    )
    in_specs = (
        P("batch", NEURON),
        P(None, NEURON, None, None),
        P(None, NEURON, None),
        P(None, NEURON),
        P(None, NEURON),
    )
    out_specs = P("batch", NEURON)
    return jax.shard_map(local, mesh=split, in_specs=in_specs, out_specs=out_specs, check_vma=False)
```

time: 144 us -> 139 us (0.965)
  blocking collectives: 111 us -> 92.1 us
  starting transfers between devices: 8.47 us -> 15.9 us
  other arithmetic: 1.53 us -> 5.85 us
  Pallas kernels: 0 us -> 1.51 us
    all_to_all x9 -> x7, blocking collectives: 111 us -> 92.1 us  [exchanged(): return lax.all_to_all(value, axes, split_axis=0, concat_axis=0, tiled=True)]
    all_to_all x1 -> x2, starting transfers between devices: 8.47 us -> 15.9 us  [exchanged(): return lax.all_to_all(value, axes, split_axis=0, concat_axis=0, tiled=True)]
    select_n x0 -> x3, other arithmetic: none -> 2.71 us  [the longest x1 1.35 us: local(): target = jnp.where(own_cols >= 0, target, -1)]
    dot_general x0 -> x2, matrix products: none -> 1.91 us  [the longest x1 1.06 us: local(): jnp.einsum('ts,isn->tin', packing, products.astype(jnp.float32), precisio...]
    slice x1 -> x2, local copies, waits for them, and re-layouts: 0.03 us -> 1.93 us  [the longest x1 1.24 us: local(): tile_count[layers - 1, 0]]
    pallas_call x0 -> x1, Pallas kernels: none -> 1.51 us  [local(): pl.pallas_call(opening_kernel, out_shape=jax.ShapeDtypeStruct((planes, ow...]
    all_to_all x1 -> x2, waiting for transfers between devices: 9.03 us -> 9.02 us  [exchanged(): return lax.all_to_all(value, axes, split_axis=0, concat_axis=0, tiled=True)]
  transfers between devices with their start and end apart: 1 -> 2, of which waited for: 1 -> 2; matrix products, arithmetic and copies ran while one was open for 0% -> 5% of each run, Pallas kernels for 0% -> 0%
where the time goes in v3:
time: 139 us; the launch traced here: 138 us
  blocking collectives  92.1 us (66%)
  starting transfers between devices  15.9 us (11%)
  matrix products  10 us (7%)
  waiting for transfers between devices  9.02 us (6%)
  other arithmetic  5.85 us (4%)
  local copies, waits for them, and re-layouts  3.64 us (3%)
  Pallas kernels  1.51 us (1%)
    all_to_all x7, blocking collectives, exchanged(): return lax.all_to_all(value, axes, split_axis=0, concat_axis=0, tiled=True)  92.1 us
    all_to_all x2, starting transfers between devices, exchanged(): return lax.all_to_all(value, axes, split_axis=0, concat_axis=0, tiled=True)  15.9 us
    all_to_all x2, waiting for transfers between devices, exchanged(): return lax.all_to_all(value, axes, split_axis=0, concat_axis=0, tiled=True)  9.02 us
    dot_general x2, matrix products, local(): jnp.einsum('isk,skn->isn', picked, tile_weights[layer], preferred_element...  4.8 us
  transfers between devices with their start and end apart: 2, of which 2 were waited for; matrix products, arithmetic and copies ran while one was open for 5% of the time, Pallas kernels for 0%

profile of v3, /device:TPU:2, one launch (start us, length us, event | category | flops | bytes accessed | tf_op | source)
XLA Modules:
  0.0 138.2 jit_solution(3542569494407323626)
XLA Ops:
  0.0 1.5 %opening.1 = f32[16,16,128]{2,1,0:T(8,128)} custom-call(s32[1,2]{1,0:T(1,128)} %bitcast.90, bf16[16,512]{1,0:T(8,128)(2,1)} %images_ref.1, s32[2,2,128]{2,1,0:T(2,128)} %bitcast.89, f32[2,512]{1,0:T(2,128)} %bias_ref.1), custom_call_target="tpu_custom_call" | custom-call | tf_op jit(solution)/shard_map/opening/pallas_call | solution.py:61
  1.5 7.5 %all-to-all-start = ((f32[16,16,128]{2,1,0:T(8,128)}), f32[16,16,128]{2,1,0:T(8,128)S(1)}, u32[]{:S(2)}, u32[]{:S(2)}) async-start(f32[16,16,128]{2,1,0:T(8,128)} %opening.1), calls=%async_computation | async-start | bytes 262144 | tf_op jit(solution)/shard_map/all_to_all | solution.py:19
  9.0 1.2 slice.40
  10.2 1.3 and_select_fusion.4
  11.6 1.3 broadcast_compare_fusion
  12.9 0.2 convert_reduce_fusion.3
  13.1 1.4 add_select_fusion
  14.5 0.7 slice.44
  15.2 0.4 all-to-all-done
  15.6 0.1 fusion.42
  15.8 0.3 convert_reduce_fusion
  16.2 0.7 broadcast_in_dim.26
  16.9 8.5 %all-to-all-start.1 = ((bf16[8,64,128]{2,1,0:T(8,128)(2,1)}), bf16[8,64,128]{2,1,0:T(8,128)(2,1)S(1)}, u32[]{:S(2)}, u32[]{:S(2)}) async-start(bf16[8,64,128]{2,1,0:T(8,128)(2,1)} %broadcast_in_dim.26), calls=%async_computation.1 | async-start | bytes 262144 | tf_op jit(solution)/shard_map/all_to_all | solution.py:19
  25.3 0.3 select_reduce_fusion
  25.7 0.1 eq.128
  25.7 0.1 compare_convert_fusion
  25.8 8.6 %all-to-all-done.1 = bf16[8,64,128]{2,1,0:T(8,128)(2,1)S(1)} async-done(((bf16[8,64,128]{2,1,0:T(8,128)(2,1)}), bf16[8,64,128]{2,1,0:T(8,128)(2,1)S(1)}, u32[]{:S(2)}, u32[]{:S(2)}) %all-to-all-start.1) | async-done | bytes 131104 | tf_op jit(solution)/shard_map/all_to_all | solution.py:19
  34.4 0.0 slice-start
  34.4 1.0 fusion.9
  35.4 15.5 %all_to_all.57 = bf16[16,128,128]{2,1,0:T(8,128)(2,1)S(1)} all-to-all(bf16[16,128,128]{2,1,0:T(8,128)(2,1)S(1)} %bitcast.73), channel_id=1, replica_groups=mesh['batch'=2,'neuron_0'=8,'neuron_1'=4,'neuron_2'=4] {'neuron_1','neur..., dimensions={0} | all-to-all | bytes 1048576 | tf_op jit(solution)/shard_map/all_to_all | solution.py:19
  51.0 0.0 slice-start.1
  51.0 3.6 %fusion.23 = f16[16,128,128]{2,0,1:T(8,128)(2,1)S(1)} fusion(bf16[2,128,128,128]{3,2,1,0:T(8,128)(2,1)} %param.6, bf16[16,128,128]{2,1,0:T(8,128)(2,1)S(1)} %all_to_all.57), kind=kOutput, calls=%fused_computation.21 | convolution fusion | flops 67371008 | bytes 5242880 | tf_op jit(solution)/shard_map/isk,skn->isn/dot_general | solution.py:100
  54.6 0.2 copy.32
  54.8 13.1 %all_to_all.58 = f16[16,128,128]{2,1,0:T(8,128)(2,1)S(1)} all-to-all(f16[16,128,128]{2,1,0:T(8,128)(2,1)S(1)} %copy.32), channel_id=1, replica_groups=mesh['batch'=2,'neuron_0'=8,'neuron_1'=4,'neuron_2'=4] {'neuron_1','neur..., dimensions={0} | all-to-all | bytes 1048576 | tf_op jit(solution)/shard_map/all_to_all | solution.py:19
  67.9 1.3 fusion.26
  69.2 11.5 %all_to_all.59 = f16[8,64,128]{2,1,0:T(8,128)(2,1)S(1)} all-to-all(f16[8,64,128]{2,1,0:T(8,128)(2,1)S(1)} %bitcast.78), channel_id=1, replica_groups=mesh['batch'=2,'neuron_0'=8,'neuron_1'=4,'neuron_2'=4] {'neuron_0'}, dimensions={0} | all-to-all | bytes 262144 | tf_op jit(solution)/shard_map/all_to_all | solution.py:19
  80.7 11.5 %all_to_all.60 = bf16[8,64,128]{2,1,0:T(8,128)(2,1)S(1)} all-to-all(bf16[8,64,128]{2,1,0:T(8,128)(2,1)S(1)} %broadcast_in_dim.31), channel_id=1, replica_groups=mesh['batch'=2,'neuron_0'=8,'neuron_1'=4,'neuron_2'=4] {'neuron_0'}, dimensions={0} | all-to-all | bytes 262144 | tf_op jit(solution)/shard_map/all_to_all | solution.py:19
  92.2 1.0 fusion.10
  93.2 13.1 %all_to_all.61 = bf16[16,128,128]{2,1,0:T(8,128)(2,1)S(1)} all-to-all(bf16[16,128,128]{2,1,0:T(8,128)(2,1)S(1)} %bitcast.75), channel_id=1, replica_groups=mesh['batch'=2,'neuron_0'=8,'neuron_1'=4,'neuron_2'=4] {'neuron_1','neur..., dimensions={0} | all-to-all | bytes 1048576 | tf_op jit(solution)/shard_map/all_to_all | solution.py:19
  106.3 0.0 slice-done
  106.3 0.0 slice-done.1
  106.3 1.2 fusion.20
  107.5 1.1 convolution_convert_fusion
  108.6 0.7 copy.35
  109.3 15.9 %all_to_all.62 = f16[256,16,128]{2,1,0:T(8,128)(2,1)S(1)} all-to-all(f16[256,16,128]{2,1,0:T(8,128)(2,1)S(1)} %copy.35), channel_id=1, replica_groups=mesh['batch'=2,'neuron_0'=8,'neuron_1'=4,'neuron_2'=4] {'neuron_1','neur..., dimensions={0} | all-to-all | bytes 2097152 | tf_op jit(solution)/shard_map/all_to_all | solution.py:19
  125.2 0.8 convolution_convert_fusion.1
  126.0 0.1 copy.37
  126.1 11.5 %all_to_all.63 = f16[32,16,128]{2,1,0:T(8,128)(2,1)S(1)} all-to-all(f16[32,16,128]{2,1,0:T(8,128)(2,1)S(1)} %copy.37), channel_id=1, replica_groups=mesh['batch'=2,'neuron_0'=8,'neuron_1'=4,'neuron_2'=4] {'neuron_0'}, dimensions={0} | all-to-all | bytes 262144 | tf_op jit(solution)/shard_map/all_to_all | solution.py:19
  137.6 0.6 fusion.34
  (12 shorter events, 0.2 us)
Async XLA Ops:
  1.5 14.1 %all-to-all-start = ((f32[16,16,128]{2,1,0:T(8,128)}), f32[16,16,128]{2,1,0:T(8,128)S(1)}, u32[]{:S(2)}, u32[]{:S(2)}) async-start(f32[16,16,128]{2,1,0:T(8,128)} %opening.1), calls=%async_computation | async-start | bytes 262144 | tf_op jit(solution)/shard_map/all_to_all | solution.py:19
  16.9 17.5 %all-to-all-start.1 = ((bf16[8,64,128]{2,1,0:T(8,128)(2,1)}), bf16[8,64,128]{2,1,0:T(8,128)(2,1)S(1)}, u32[]{:S(2)}, u32[]{:S(2)}) async-start(bf16[8,64,128]{2,1,0:T(8,128)(2,1)} %broadcast_in_dim.26), calls=%async_computation.1 | async-start | bytes 262144 | tf_op jit(solution)/shard_map/all_to_all | solution.py:19
  34.4 71.9 %slice-start = ((s8[8388608]{0:T(1024)(128)(4,1)}), s8[4194304]{0:T(1024)(128)(4,1)S(1)}, s32[]{:S(2)}) async-start(s8[8388608]{0:T(1024)(128)(4,1)} %bitcast.70), calls=%async_computation.9 | async-start | bytes 8388608
  51.0 55.3 %slice-start.1 = ((s8[8388608]{0:T(1024)(128)(4,1)}), s8[4194304]{0:T(1024)(128)(4,1)S(1)}, s32[]{:S(2)}) async-start(s8[8388608]{0:T(1024)(128)(4,1)} %bitcast.70), calls=%async_computation.10 | async-start | bytes 8388608

commit v4 on v3

--- a/solution.py
+++ b/solution.py
@@ -70,9 +70,9 @@
     routes = opened[:, own : own + layers * 2].astype(jnp.int32)
     biases = opened[:, own + layers * 2 :]
 
-    own_cols = jnp.where(
-        jnp.arange(slots, dtype=jnp.int32) < tile_count[layers - 1, 0], tile_blocks[layers - 1, :, 1], -every
-    )
+    own_row = lax.dynamic_index_in_dim(opened, me, axis=0, keepdims=False)
+    own_cols = own_row[own + layers * 2 - 1].astype(jnp.int32)
+    last_bias = own_row[own + layers * 2 + (layers - 1) * own :]
     plane = (own_cols // own) % planes
     same = (plane[:, None] == plane[None, :]) & (own_cols >= 0)[None, :]
     earlier = jnp.arange(slots)[None, :] < jnp.arange(slots)[:, None]
@@ -87,7 +87,6 @@
 
     packing = (jnp.arange(planes * room, dtype=jnp.int32)[:, None] == target[None, :]).astype(jnp.float32)
     chosen = (jnp.arange(1, heights * own + 1, dtype=jnp.int32)[:, None] == labels[None, :]).astype(jnp.float32)
-    last_bias = bias[layers - 1]
 
     for layer in range(layers):
         spread = jnp.broadcast_to(state[None], (heights, held, width)).reshape(every, width)
@@ -116,8 +115,9 @@
     got = exchanged(packed.astype(WIRE), PLANE)
     middle = jnp.einsum("or,rin->oin", chosen, got.astype(jnp.float32), precision=lax.Precision.HIGH)
     ended = exchanged(middle.astype(WIRE), HEIGHT).reshape(heights, own, rows, width)
-    summed = jnp.sum(ended.astype(jnp.float32), axis=0).transpose(1, 0, 2).reshape(rows, local_width)
-    return jnp.clip(summed + last_bias[None, :], 0.0, CEILING).astype(jnp.bfloat16)
+    summed = jnp.sum(ended.astype(jnp.float32), axis=0) + last_bias[:, None, :]
+    activity = jnp.clip(summed, 0.0, CEILING).astype(jnp.bfloat16)
+    return activity.transpose(1, 0, 2).reshape(rows, local_width)
 
 
 def solution(mesh):

time: 139 us -> 137 us (0.986)
  waiting for transfers between devices: 9.02 us -> 15.3 us
  other arithmetic: 5.85 us -> 1.89 us
  blocking collectives: 92.1 us -> 89.9 us
  local copies, waits for them, and re-layouts: 3.64 us -> 1.73 us
    all_to_all x2, waiting for transfers between devices: 9.02 us -> 15.3 us  [exchanged(): return lax.all_to_all(value, axes, split_axis=0, concat_axis=0, tiled=True)]
    all_to_all x7, blocking collectives: 92.1 us -> 89.9 us  [exchanged(): return lax.all_to_all(value, axes, split_axis=0, concat_axis=0, tiled=True)]
    slice x2 -> x1, local copies, waits for them, and re-layouts: 1.93 us -> 0.01 us  [local(): last_bias = own_row[own + layers * 2 + (layers - 1) * own:]]
  transfers between devices with their start and end apart: 2 -> 2, of which waited for: 2 -> 2; matrix products, arithmetic and copies ran while one was open for 5% -> 0% of each run, Pallas kernels for 0% -> 0%
where the time goes in v4:
time: 137 us; the launch traced here: 136 us
  blocking collectives  89.9 us (66%)
  starting transfers between devices  15.9 us (12%)
  waiting for transfers between devices  15.3 us (11%)
  matrix products  10 us (7%)
  other arithmetic  1.89 us (1%)
  local copies, waits for them, and re-layouts  1.73 us (1%)
  Pallas kernels  1.51 us (1%)
    all_to_all x7, blocking collectives, exchanged(): return lax.all_to_all(value, axes, split_axis=0, concat_axis=0, tiled=True)  89.9 us
    all_to_all x2, starting transfers between devices, exchanged(): return lax.all_to_all(value, axes, split_axis=0, concat_axis=0, tiled=True)  15.9 us
    all_to_all x2, waiting for transfers between devices, exchanged(): return lax.all_to_all(value, axes, split_axis=0, concat_axis=0, tiled=True)  15.3 us
    dot_general x2, matrix products, local(): jnp.einsum('isk,skn->isn', picked, tile_weights[layer], preferred_element...  4.8 us
  transfers between devices with their start and end apart: 2, of which 2 were waited for; matrix products, arithmetic and copies ran while one was open for 0% of the time, Pallas kernels for 0%

profile of v4, /device:TPU:2, one launch (start us, length us, event | category | flops | bytes accessed | tf_op | source)
XLA Modules:
  0.0 136.5 jit_solution(9594181368615216852)
XLA Ops:
  0.0 1.5 %opening.1 = f32[16,16,128]{2,1,0:T(8,128)} custom-call(s32[1,2]{1,0:T(1,128)} %bitcast.85, bf16[16,512]{1,0:T(8,128)(2,1)} %images_ref.1, s32[2,2,128]{2,1,0:T(2,128)} %bitcast.84, f32[2,512]{1,0:T(2,128)} %bias_ref.1), custom_call_target="tpu_custom_call" | custom-call | tf_op jit(solution)/shard_map/opening/pallas_call | solution.py:61
  1.5 7.5 %all-to-all-start = ((f32[16,16,128]{2,1,0:T(8,128)}), f32[16,16,128]{2,1,0:T(8,128)S(1)}, u32[]{:S(2)}, u32[]{:S(2)}) async-start(f32[16,16,128]{2,1,0:T(8,128)} %opening.1), calls=%async_computation | async-start | bytes 262144 | tf_op jit(solution)/shard_map/all_to_all | solution.py:19
  9.0 6.6 %all-to-all-done = f32[16,16,128]{2,1,0:T(8,128)S(1)} async-done(((f32[16,16,128]{2,1,0:T(8,128)}), f32[16,16,128]{2,1,0:T(8,128)S(1)}, u32[]{:S(2)}, u32[]{:S(2)}) %all-to-all-start) | async-done | bytes 131104 | tf_op jit(solution)/shard_map/all_to_all | solution.py:19
  15.6 0.1 fusion.42
  15.8 0.3 convert_reduce_fusion
  16.2 0.3 select_reduce_fusion
  16.5 0.1 eq.128
  16.6 0.7 broadcast_in_dim.19
  17.3 8.5 %all-to-all-start.1 = ((bf16[8,64,128]{2,1,0:T(8,128)(2,1)}), bf16[8,64,128]{2,1,0:T(8,128)(2,1)S(1)}, u32[]{:S(2)}, u32[]{:S(2)}) async-start(bf16[8,64,128]{2,1,0:T(8,128)(2,1)} %broadcast_in_dim.19), calls=%async_computation.1 | async-start | bytes 262144 | tf_op jit(solution)/shard_map/all_to_all | solution.py:19
  25.8 0.2 convert_reduce_fusion.3
  26.0 0.1 compare_convert_fusion
  26.1 8.7 %all-to-all-done.1 = bf16[8,64,128]{2,1,0:T(8,128)(2,1)S(1)} async-done(((bf16[8,64,128]{2,1,0:T(8,128)(2,1)}), bf16[8,64,128]{2,1,0:T(8,128)(2,1)S(1)}, u32[]{:S(2)}, u32[]{:S(2)}) %all-to-all-start.1) | async-done | bytes 131104 | tf_op jit(solution)/shard_map/all_to_all | solution.py:19
  34.8 0.0 slice-start
  34.8 1.0 fusion.9
  35.9 13.3 %all_to_all.57 = bf16[16,128,128]{2,1,0:T(8,128)(2,1)S(1)} all-to-all(bf16[16,128,128]{2,1,0:T(8,128)(2,1)S(1)} %bitcast.69), channel_id=1, replica_groups=mesh['batch'=2,'neuron_0'=8,'neuron_1'=4,'neuron_2'=4] {'neuron_1','neur..., dimensions={0} | all-to-all | bytes 1048576 | tf_op jit(solution)/shard_map/all_to_all | solution.py:19
  49.2 0.0 slice-start.1
  49.2 3.6 %fusion.23 = f16[16,128,128]{2,0,1:T(8,128)(2,1)S(1)} fusion(bf16[2,128,128,128]{3,2,1,0:T(8,128)(2,1)} %param.6, bf16[16,128,128]{2,1,0:T(8,128)(2,1)S(1)} %all_to_all.57), kind=kOutput, calls=%fused_computation.21 | convolution fusion | flops 67371008 | bytes 5242880 | tf_op jit(solution)/shard_map/isk,skn->isn/dot_general | solution.py:99
  52.8 0.2 copy.32
  53.0 13.1 %all_to_all.58 = f16[16,128,128]{2,1,0:T(8,128)(2,1)S(1)} all-to-all(f16[16,128,128]{2,1,0:T(8,128)(2,1)S(1)} %copy.32), channel_id=1, replica_groups=mesh['batch'=2,'neuron_0'=8,'neuron_1'=4,'neuron_2'=4] {'neuron_1','neur..., dimensions={0} | all-to-all | bytes 1048576 | tf_op jit(solution)/shard_map/all_to_all | solution.py:19
  66.1 1.3 fusion.26
  67.4 11.5 %all_to_all.59 = f16[8,64,128]{2,1,0:T(8,128)(2,1)S(1)} all-to-all(f16[8,64,128]{2,1,0:T(8,128)(2,1)S(1)} %bitcast.74), channel_id=1, replica_groups=mesh['batch'=2,'neuron_0'=8,'neuron_1'=4,'neuron_2'=4] {'neuron_0'}, dimensions={0} | all-to-all | bytes 262144 | tf_op jit(solution)/shard_map/all_to_all | solution.py:19
  78.9 11.5 %all_to_all.60 = bf16[8,64,128]{2,1,0:T(8,128)(2,1)S(1)} all-to-all(bf16[8,64,128]{2,1,0:T(8,128)(2,1)S(1)} %broadcast_in_dim.27), channel_id=1, replica_groups=mesh['batch'=2,'neuron_0'=8,'neuron_1'=4,'neuron_2'=4] {'neuron_0'}, dimensions={0} | all-to-all | bytes 262144 | tf_op jit(solution)/shard_map/all_to_all | solution.py:19
  90.4 1.0 fusion.10
  91.4 13.1 %all_to_all.61 = bf16[16,128,128]{2,1,0:T(8,128)(2,1)S(1)} all-to-all(bf16[16,128,128]{2,1,0:T(8,128)(2,1)S(1)} %bitcast.71), channel_id=1, replica_groups=mesh['batch'=2,'neuron_0'=8,'neuron_1'=4,'neuron_2'=4] {'neuron_1','neur..., dimensions={0} | all-to-all | bytes 1048576 | tf_op jit(solution)/shard_map/all_to_all | solution.py:19
  104.5 0.0 slice-done
  104.5 0.0 slice-done.1
  104.5 1.2 fusion.20
  105.7 1.1 convolution_convert_fusion
  106.8 0.7 copy.35
  107.5 15.9 %all_to_all.62 = f16[256,16,128]{2,1,0:T(8,128)(2,1)S(1)} all-to-all(f16[256,16,128]{2,1,0:T(8,128)(2,1)S(1)} %copy.35), channel_id=1, replica_groups=mesh['batch'=2,'neuron_0'=8,'neuron_1'=4,'neuron_2'=4] {'neuron_1','neur..., dimensions={0} | all-to-all | bytes 2097152 | tf_op jit(solution)/shard_map/all_to_all | solution.py:19
  123.4 0.8 convolution_convert_fusion.1
  124.3 0.1 copy.37
  124.4 11.5 %all_to_all.63 = f16[32,16,128]{2,1,0:T(8,128)(2,1)S(1)} all-to-all(f16[32,16,128]{2,1,0:T(8,128)(2,1)S(1)} %copy.37), channel_id=1, replica_groups=mesh['batch'=2,'neuron_0'=8,'neuron_1'=4,'neuron_2'=4] {'neuron_0'}, dimensions={0} | all-to-all | bytes 262144 | tf_op jit(solution)/shard_map/all_to_all | solution.py:19
  135.8 0.6 copy_bitcast_fusion
  (16 shorter events, 0.2 us)
Async XLA Ops:
  1.5 14.1 %all-to-all-start = ((f32[16,16,128]{2,1,0:T(8,128)}), f32[16,16,128]{2,1,0:T(8,128)S(1)}, u32[]{:S(2)}, u32[]{:S(2)}) async-start(f32[16,16,128]{2,1,0:T(8,128)} %opening.1), calls=%async_computation | async-start | bytes 262144 | tf_op jit(solution)/shard_map/all_to_all | solution.py:19
  17.3 17.5 %all-to-all-start.1 = ((bf16[8,64,128]{2,1,0:T(8,128)(2,1)}), bf16[8,64,128]{2,1,0:T(8,128)(2,1)S(1)}, u32[]{:S(2)}, u32[]{:S(2)}) async-start(bf16[8,64,128]{2,1,0:T(8,128)(2,1)} %broadcast_in_dim.19), calls=%async_computation.1 | async-start | bytes 262144 | tf_op jit(solution)/shard_map/all_to_all | solution.py:19
  34.8 69.7 %slice-start = ((s8[8388608]{0:T(1024)(128)(4,1)}), s8[4194304]{0:T(1024)(128)(4,1)S(1)}, s32[]{:S(2)}) async-start(s8[8388608]{0:T(1024)(128)(4,1)} %bitcast.66), calls=%async_computation.9 | async-start | bytes 8388608
  49.2 55.3 %slice-start.1 = ((s8[8388608]{0:T(1024)(128)(4,1)}), s8[4194304]{0:T(1024)(128)(4,1)S(1)}, s32[]{:S(2)}) async-start(s8[8388608]{0:T(1024)(128)(4,1)} %bitcast.66), calls=%async_computation.10 | async-start | bytes 8388608
